TPU v7x, 8 devices: a whole 2x2x1 slice. The times are simulated.
8 devices in a mesh: dp: 1 (over z), tp: 8 (over y, x, core).
Axes of the slice: x: 2, y: 2, z: 1, core: 2. Of those that a mesh axis runs over, the one named last changes fastest.
Arguments:
- y_one: float32 [16, 256, 1024], P('dp')
- y_two: float32 [16, 256, 1024], P('dp')
- dy_one: float32 [16, 256, 1024], P('dp')
- dy_two: float32 [16, 256, 1024], P('dp')
- saved_one: float32 [2, 16, 256, 1024], P(None, 'dp')
- saved_two: float32 [2, 16, 256, 1024], P(None, 'dp')
- w_qkv: bfloat16 [5, 1024, 3, 16, 64], P(None, None, None, 'tp')
- w_o: bfloat16 [5, 16, 64, 1024], P(None, 'tp')
- w_in: bfloat16 [5, 1024, 4096], P(None, None, 'tp')
- w_out: bfloat16 [5, 4096, 1024], P(None, 'tp')
Outputs:
- output 1: float32 [16, 256, 1024], P('dp')
- output 2: float32 [16, 256, 1024], P('dp')
- output 3: float32 [16, 256, 1024], P('dp')
- output 4: float32 [16, 256, 1024], P('dp')
- output 5: float32 [5, 1024, 3, 16, 64], P('dp', None, None, 'tp')
- output 6: float32 [5, 16, 64, 1024], P('dp', 'tp')
- output 7: float32 [5, 1024, 4096], P('dp', None, 'tp')
- output 8: float32 [5, 4096, 1024], P('dp', 'tp')
All inputs are finite; a program needn't handle non-finite values.
Results may differ from a plain program's by a relative error of at most 0.0127618.
Values are sent between devices in bfloat16 or wider.
A program may use at most 1 GiB of HBM per device.

v0:
```python
import jax
import jax.numpy as jnp
from jax import lax
from jax.sharding import PartitionSpec as P

EPS = 1e-6


def rms_norm(state):
    return state * lax.rsqrt(jnp.mean(state * state, axis=-1, keepdims=True) + EPS)


def gelu_tanh(hidden):
    return jax.nn.gelu(hidden, approximate=True)


def attn_forward(normed, w_qkv):
    head_dim = w_qkv.shape[-1]
    qkv_all = jnp.einsum("bsh,hkne->kbsne", normed, w_qkv, preferred_element_type=jnp.float32).astype(jnp.bfloat16)
    scores = jnp.einsum("bqne,bkne->bnqk", qkv_all[0], qkv_all[1], preferred_element_type=jnp.float32) * head_dim ** -0.5
    attn_probs = jax.nn.softmax(scores, axis=-1)
    probs_bf = attn_probs.astype(jnp.bfloat16)
    heads_out = jnp.einsum("bnqk,bkne->bqne", probs_bf, qkv_all[2], preferred_element_type=jnp.float32).astype(jnp.bfloat16)
    return qkv_all, attn_probs, probs_bf, heads_out


def attn_backward(normed, w_qkv, w_o, attn_cache, d_out):
    qkv_all, attn_probs, probs_bf, heads_out = attn_cache
    head_dim = w_qkv.shape[-1]
    d_bf = d_out.astype(jnp.bfloat16)
    d_wo = jnp.einsum("bqne,bqh->neh", heads_out, d_bf, preferred_element_type=jnp.float32)
    d_heads = jnp.einsum("bqh,neh->bqne", d_bf, w_o, preferred_element_type=jnp.float32).astype(jnp.bfloat16)
    d_v = jnp.einsum("bnqk,bqne->bkne", probs_bf, d_heads, preferred_element_type=jnp.float32)
    d_probs = jnp.einsum("bqne,bkne->bnqk", d_heads, qkv_all[2], preferred_element_type=jnp.float32)
    d_scores = attn_probs * (d_probs - jnp.sum(d_probs * attn_probs, axis=-1, keepdims=True)) * head_dim ** -0.5
    ds_bf = d_scores.astype(jnp.bfloat16)
    d_q = jnp.einsum("bnqk,bkne->bqne", ds_bf, qkv_all[1], preferred_element_type=jnp.float32)
    d_k = jnp.einsum("bnqk,bqne->bkne", ds_bf, qkv_all[0], preferred_element_type=jnp.float32)
    d_qkv = jnp.stack([d_q.astype(jnp.bfloat16), d_k.astype(jnp.bfloat16), d_v.astype(jnp.bfloat16)], axis=2)
    d_wqkv = jnp.einsum("bsh,bskne->hkne", normed, d_qkv, preferred_element_type=jnp.float32)
    d_normed = jnp.einsum("bskne,hkne->bsh", d_qkv, w_qkv, preferred_element_type=jnp.float32)
    return d_normed, d_wqkv, d_wo


def mlp_forward(normed, w_in):
    hidden = jnp.einsum("bsh,hf->bsf", normed, w_in, preferred_element_type=jnp.float32)
    gelu_out, gelu_pull = jax.vjp(gelu_tanh, hidden)
    return gelu_out.astype(jnp.bfloat16), gelu_pull


def mlp_backward(normed, w_in, w_out, act_bf, gelu_pull, d_out):
    d_bf = d_out.astype(jnp.bfloat16)
    d_wout = jnp.einsum("bsf,bsh->fh", act_bf, d_bf, preferred_element_type=jnp.float32)
    d_act = jnp.einsum("bsh,fh->bsf", d_bf, w_out, preferred_element_type=jnp.float32)
    d_hidden = gelu_pull(d_act)[0].astype(jnp.bfloat16)
    d_win = jnp.einsum("bsh,bsf->hf", normed, d_hidden, preferred_element_type=jnp.float32)
    d_normed = jnp.einsum("bsf,hf->bsh", d_hidden, w_in, preferred_element_type=jnp.float32)
    return d_normed, d_win, d_wout


def reversible_block(block_w, y_one, y_two, d_one, d_two, want_x_one):
    w_qkv, w_o, w_in, w_out = block_w
    g_norm, g_norm_pull = jax.vjp(rms_norm, y_one)
    g_in = g_norm.astype(jnp.bfloat16)
    act_bf, gelu_pull = mlp_forward(g_in, w_in)
    g_part = jnp.einsum("bsf,fh->bsh", act_bf, w_out, preferred_element_type=jnp.float32)
    x_two = y_two - lax.psum(g_part, "tp")
    g_back, d_win, d_wout = mlp_backward(g_in, w_in, w_out, act_bf, gelu_pull, d_two)
    d_one = d_one + g_norm_pull(lax.psum(g_back, "tp"))[0]
    f_norm, f_norm_pull = jax.vjp(rms_norm, x_two)
    f_in = f_norm.astype(jnp.bfloat16)
    attn_cache = attn_forward(f_in, w_qkv)
    x_one = None
    if want_x_one:
        f_part = jnp.einsum("bqne,neh->bqh", attn_cache[3], w_o, preferred_element_type=jnp.float32)
        x_one = y_one - lax.psum(f_part, "tp")
    f_back, d_wqkv, d_wo = attn_backward(f_in, w_qkv, w_o, attn_cache, d_one)
    d_two = d_two + f_norm_pull(lax.psum(f_back, "tp"))[0]
    return x_one, x_two, d_one, d_two, (d_wqkv, d_wo, d_win, d_wout)


def plain_block(block_w, x_one, x_two, d_one, d_two):
    w_qkv, w_o, w_in, w_out = block_w
    f_norm, f_norm_pull = jax.vjp(rms_norm, x_two)
    f_in = f_norm.astype(jnp.bfloat16)
    attn_cache = attn_forward(f_in, w_qkv)
    f_back, d_wqkv, d_wo = attn_backward(f_in, w_qkv, w_o, attn_cache, d_one)
    g_norm, g_norm_pull = jax.vjp(rms_norm, x_one)
    g_in = g_norm.astype(jnp.bfloat16)
    act_bf, gelu_pull = mlp_forward(g_in, w_in)
    g_back, d_win, d_wout = mlp_backward(g_in, w_in, w_out, act_bf, gelu_pull, d_two)
    new_one = d_one + g_norm_pull(lax.psum(g_back, "tp"))[0]
    new_two = d_two + f_norm_pull(lax.psum(f_back, "tp"))[0]
    return new_one, new_two, (d_wqkv, d_wo, d_win, d_wout)


def solution(mesh):
    act_spec = P("dp", None, None)
    saved_spec = P(None, "dp", None, None)
    weight_specs = (P(None, None, None, "tp", None), P(None, "tp", None, None), P(None, None, "tp"), P(None, "tp", None))
    grad_specs = (P("dp", None, None, "tp", None), P("dp", "tp", None, None), P("dp", None, "tp"), P("dp", "tp", None))

    def per_device(y_one, y_two, dy_one, dy_two, saved_one, saved_two, w_qkv, w_o, w_in, w_out):
        all_w = (w_qkv, w_o, w_in, w_out)
        n_layers = w_qkv.shape[0]
        n_pairs = saved_one.shape[0]
        grad_list = [None] * n_layers
        top_w = tuple(weight[n_layers - 1] for weight in all_w)
        x_one, x_two, d_one, d_two, top_grads = reversible_block(top_w, y_one, y_two, dy_one, dy_two, n_pairs == 0)
        grad_list[n_layers - 1] = top_grads
        for pair_idx in reversed(range(n_pairs)):
            plain_w = tuple(weight[2 * pair_idx + 1] for weight in all_w)
            d_one, d_two, plain_grads = plain_block(plain_w, saved_one[pair_idx], saved_two[pair_idx], d_one, d_two)
            grad_list[2 * pair_idx + 1] = plain_grads
            rev_w = tuple(weight[2 * pair_idx] for weight in all_w)
            x_one, x_two, d_one, d_two, rev_grads = reversible_block(rev_w, saved_one[pair_idx], saved_two[pair_idx], d_one, d_two, pair_idx == 0)
            grad_list[2 * pair_idx] = rev_grads
        stacked = tuple(jnp.stack([entry[slot_idx] for entry in grad_list]) for slot_idx in range(4))
        return (x_one, x_two, d_one, d_two) + stacked

    return jax.shard_map(
        per_device,
        mesh=mesh,
        in_specs=(act_spec,) * 4 + (saved_spec,) * 2 + weight_specs,
        out_specs=(act_spec,) * 4 + grad_specs,
        check_vma=False,
    )
```

profile of v0, /device:TPU:0, one launch (start us, length us, event | category | flops | bytes accessed | tf_op | source)
XLA Modules:
  0.0 3539.6 jit_solution(11115235807073408525)
XLA Ops:
  33.9 13.4 fusion.47
  90.2 358.8 %all-reduce.23.cloned.1.call-done = (f32[16,256,1024]{2,1,0:T(8,128)}, f32[16,256,1024]{2,1,0:T(8,128)}) async-done(((f32[16,256,1024]{2,1,0:T(8,128)}, f32[16,256,1024]{2,1,0:T(8,128)}), (f32[16,256,1024]{2,1,0:T(8,128)}, f32[16,256,1024]{2,1,0:T(8,128)})) %all-reduce.23.cloned.1.call-update) | async-done | bytes 33554448 | tf_op jit(solution)/shard_map/psum | solution.py:67
  448.9 27.6 multiply_reduce_fusion.4
  476.6 23.4 fusion.581
  512.9 13.4 fusion.344
  526.3 14.7 fusion.347
  567.5 14.4 fusion.341
  581.9 14.4 fusion.338
  661.1 350.0 %all-reduce.21.cloned.1.call-done = (f32[16,256,1024]{2,1,0:T(8,128)}, f32[16,256,1024]{2,1,0:T(8,128)}) async-done(((f32[16,256,1024]{2,1,0:T(8,128)}, f32[16,256,1024]{2,1,0:T(8,128)}), (f32[16,256,1024]{2,1,0:T(8,128)}, f32[16,256,1024]{2,1,0:T(8,128)})) %all-reduce.21.cloned.1.call-update) | async-done | bytes 33554448 | tf_op jit(solution)/shard_map/psum | solution.py:78
  1038.2 36.3 %fusion.14 = (f32[16,256,1024]{2,1,0:T(8,128)}, bf16[16,256,1024]{2,1,0:T(8,128)(2,1)}) fusion(f32[16,256,1024]{2,1,0:T(8,128)} %get-tuple-element.26, f32[2,16,256,1024]{3,2,1,0:T(8,128)} %param.15, f32[16,256]{1,0:T(8,128)S(1)} %multiply_multiply_fusion.16, f32[16,256]{1,0:T(8,128)S(1)} %copy-done.40, f32[16,256,1024]{2,1,0:T(8,128)} %param.13, ...), kind=kLoop, calls=%fused_computation.24 | loop fusion | flops 46137344 | bytes 109117440 | tf_op jit(solution)/shard_map/add | solution.py:93
  1074.6 14.7 fusion.61
  1147.8 543.4 %all-reduce.19.cloned.1.call-done = (f32[16,256,1024]{2,1,0:T(8,128)}, f32[16,256,1024]{2,1,0:T(8,128)}, f32[16,256,1024]{2,1,0:T(8,128)}) async-done(((f32[16,256,1024]{2,1,0:T(8,128)}, f32[16,256,1024]{2,1,0:T(8,128)}, f32[16,256,1024]{2,1,0:T(8,128)}), (f32[16,256,1024]{2,1,0:T(8,128)}, f32[16,256,1024]{2,1,0:T(8,128)}, f32[16,256,1024]{2,1,0:T(8,128)})) %all-reduce.19.cloned.1.call-update) | async-done | bytes 50331664 | tf_op jit(solution)/shard_map/psum | solution.py:92
  1691.2 22.1 fusion.24
  1713.3 31.8 fusion.578
  1757.3 14.4 fusion.359
  1771.8 14.4 fusion.356
  1830.5 13.4 fusion.353
  1843.9 13.8 fusion.350
  1915.8 355.9 %all-reduce.17.cloned.1.call-done = (f32[16,256,1024]{2,1,0:T(8,128)}, f32[16,256,1024]{2,1,0:T(8,128)}) async-done(((f32[16,256,1024]{2,1,0:T(8,128)}, f32[16,256,1024]{2,1,0:T(8,128)}), (f32[16,256,1024]{2,1,0:T(8,128)}, f32[16,256,1024]{2,1,0:T(8,128)})) %all-reduce.17.cloned.1.call-update) | async-done | bytes 33554448 | tf_op jit(solution)/shard_map/psum | solution.py:78
  2294.4 36.3 %fusion.18 = (f32[16,256,1024]{2,1,0:T(8,128)}, bf16[16,256,1024]{2,1,0:T(8,128)(2,1)}) fusion(f32[16,256,1024]{2,1,0:T(8,128)} %get-tuple-element.21, f32[2,16,256,1024]{3,2,1,0:T(8,128)} %param.15, f32[16,256]{1,0:T(8,128)S(1)} %multiply_multiply_fusion.12, f32[16,256]{1,0:T(8,128)S(1)} %copy-done.43, f32[16,256,1024]{2,1,0:T(8,128)} %get-tuple-element.37, ...), kind=kLoop, calls=%fused_computation.28 | loop fusion | flops 46137344 | bytes 109117440 | tf_op jit(solution)/shard_map/add | solution.py:93
  2330.7 15.1 fusion.40
  2345.9 13.7 fusion.68
  2429.0 14.3 bitcast_dynamic-update-slice_fusion.4
  2453.0 14.1 bitcast_dynamic-update-slice_fusion.2
  2467.1 479.4 %all-reduce.15.cloned.1.call-done = (f32[16,256,1024]{2,1,0:T(8,128)}, f32[16,256,1024]{2,1,0:T(8,128)}, f32[16,256,1024]{2,1,0:T(8,128)}) async-done(((f32[16,256,1024]{2,1,0:T(8,128)}, f32[16,256,1024]{2,1,0:T(8,128)}, f32[16,256,1024]{2,1,0:T(8,128)}), (f32[16,256,1024]{2,1,0:T(8,128)}, f32[16,256,1024]{2,1,0:T(8,128)}, f32[16,256,1024]{2,1,0:T(8,128)})) %all-reduce.15.cloned.1.call-update) | async-done | bytes 50331664 | tf_op jit(solution)/shard_map/psum | solution.py:67
  2979.7 19.5 fusion.31
  2999.3 28.9 fusion.17
  3042.4 14.5 fusion.365
  3056.9 14.4 fusion.362
  3220.8 261.4 %all-reduce.13.cloned.1.call-done = (f32[16,256,1024]{2,1,0:T(8,128)}, f32[16,256,1024]{2,1,0:T(8,128)}) async-done(((f32[16,256,1024]{2,1,0:T(8,128)}, f32[16,256,1024]{2,1,0:T(8,128)}), (f32[16,256,1024]{2,1,0:T(8,128)}, f32[16,256,1024]{2,1,0:T(8,128)})) %all-reduce.13.cloned.1.call-update) | async-done | bytes 33554448 | tf_op jit(solution)/shard_map/psum | solution.py:76
  3497.5 17.7 fusion.19
  3515.2 17.1 bitcast_subtract_fusion.2
  (308 shorter events, 687.0 us)
Async XLA Ops:
  7.2 441.8 %all-reduce.23.cloned.1.call-start = ((), (), s32[]{:S(2)}) async-start(), calls=%async_computation.5 | async-start | bytes 67108864 | tf_op jit(solution)/shard_map/psum | solution.py:67
  14.2 462.4 %copy-start.50 = (f32[16,256]{1,0:T(8,128)}, f32[16,256]{1,0:T(8,128)S(1)}, u32[]{:S(2)}) copy-start(f32[16,256]{1,0:T(8,128)S(1)} %fusion.520) | copy-start | bytes 49156
  59.1 952.0 %all-reduce.21.cloned.1.call-start = ((), (), s32[]{:S(2)}) async-start(), calls=%async_computation.4 | async-start | bytes 67108864 | tf_op jit(solution)/shard_map/psum | solution.py:78
  526.3 77.4 %copy-start.66 = (bf16[16,256,1,2,64]{1,4,3,0,2:T(8,128)(2,1)}, bf16[16,256,1,2,64]{1,4,3,0,2:T(8,128)(2,1)S(1)}, u32[]{:S(2)}) copy-start(bf16[16,256,1,2,64]{1,4,3,0,2:T(8,128)(2,1)S(1)} %fusion.344) | copy-start | bytes 3145732
  547.3 490.9 %copy-start.41 = (f32[16,256]{1,0:T(8,128)}, f32[16,256]{1,0:T(8,128)S(1)}, u32[]{:S(2)}) copy-start(f32[16,256]{1,0:T(8,128)S(1)} %fusion.521) | copy-start | bytes 49156
  600.9 13.5 copy-start.7
  624.2 1067.0 %all-reduce.19.cloned.1.call-start = ((), (), s32[]{:S(2)}) async-start(), calls=%async_computation.3 | async-start | bytes 100663296 | tf_op jit(solution)/shard_map/psum | solution.py:92
  631.2 19.5 copy-start.47
  1011.1 14.3 slice-start.10
  1011.1 15.5 slice-start.11
  1038.2 85.7 %copy-start.29 = (f32[16,256]{1,0:T(8,128)}, f32[16,256]{1,0:T(8,128)S(1)}, u32[]{:S(2)}) copy-start(f32[16,256]{1,0:T(8,128)S(1)} %get-tuple-element.10) | copy-start | bytes 49156
  1123.8 1148.0 %all-reduce.17.cloned.1.call-start = ((), (), s32[]{:S(2)}) async-start(), calls=%async_computation.2 | async-start | bytes 67108864 | tf_op jit(solution)/shard_map/psum | solution.py:78
  1691.2 22.2 copy-start.36
  1691.2 22.2 copy-start.48
  1843.9 31.5 copy-start.74
  1857.7 17.7 copy-start.76
  1884.8 1061.8 %all-reduce.15.cloned.1.call-start = ((), (), s32[]{:S(2)}) async-start(), calls=%async_computation.1 | async-start | bytes 100663296 | tf_op jit(solution)/shard_map/psum | solution.py:67
  2271.8 13.1 slice-start.5
  2271.8 14.3 slice-start.6
  2271.8 15.5 slice-start.7
  2330.7 15.1 copy-start.12
  2345.8 23.9 copy-start.63
  2379.2 1102.9 %all-reduce.13.cloned.1.call-start = ((), (), s32[]{:S(2)}) async-start(), calls=%async_computation | async-start | bytes 67108864 | tf_op jit(solution)/shard_map/psum | solution.py:76
  2417.0 26.3 slice-start.12
  2429.0 14.3 slice-start.13
  2979.7 61.8 %copy-start.13 = (f32[16,2,256,256]{2,3,1,0:T(8,128)}, f32[16,2,256,256]{2,3,1,0:T(8,128)S(1)}, u32[]{:S(2)}) copy-start(f32[16,2,256,256]{2,3,1,0:T(8,128)S(1)} %get-tuple-element.56) | copy-start | bytes 25165828
  2979.7 19.5 copy-start.28
  3095.8 24.9 slice-start.14
  3192.4 22.0 slice-start
  3192.4 22.0 slice-start.1
  3482.1 15.4 copy-start.2
  3482.1 15.4 copy-start.54
  (70 other events, 579.2 us)
Sparse Core Ops, SparseCore 0:
  59.3 389.6 all-reduce.22
  624.3 386.7 all-reduce.20
  1123.9 567.1 all-reduce.18
  1884.9 386.8 all-reduce.16
  2379.4 567.1 all-reduce.14
  3095.3 386.8 all-reduce.12
where the time goes:
time: 3550 us; the launch traced here: 3540 us
  waiting for transfers between devices  2350 us (66%)
  matrix products  738 us (21%)
  other arithmetic  404 us (11%)
    psum x2, waiting for transfers between devices, reversible_block(): x_two = y_two - lax.psum(g_part, 'tp')  838 us
    psum x2, waiting for transfers between devices, reversible_block(): d_two = d_two + f_norm_pull(lax.psum(f_back, 'tp'))[0]  706 us
    psum x1, waiting for transfers between devices, plain_block(): new_one = d_one + g_norm_pull(lax.psum(g_back, 'tp'))[0]  543 us
    psum x1, waiting for transfers between devices, reversible_block(): x_one = y_one - lax.psum(f_part, 'tp')  261 us
    reduce_sum x6, other arithmetic, rms_norm(): state * lax.rsqrt(jnp.mean(state * state, axis=-1, keepdims=True) + EPS)  83.1 us
    reduce_sum x7, other arithmetic, rms_norm(): jnp.mean(state * state, axis=-1, keepdims=True) + EPS  82.8 us
    add x2, other arithmetic, plain_block(): new_two = d_two + f_norm_pull(lax.psum(f_back, 'tp'))[0]  72.6 us
    dot_general x5, matrix products, attn_backward(): jnp.einsum('bnqk,bkne->bqne', ds_bf, qkv_all[1], preferred_element_type=j...  71.4 us
  transfers between devices with their start and end apart: 6, of which 6 were waited for; matrix products, arithmetic and copies ran while one was open for 9% of the time, Pallas kernels for 0%

commit v1 on v0

v1 whole, which is shorter than its diff:
```python
import functools

import jax
import jax.numpy as jnp
from jax import lax
from jax.experimental import pallas as pl
from jax.experimental.pallas import tpu as pltpu
from jax.sharding import PartitionSpec as P

EPS = 1e-6
BF = jnp.bfloat16
F32 = jnp.float32
N = 8
VMEM = 60 * 1024 * 1024


def dot(a, b):
    return lax.dot_general(a, b, (((1,), (0,)), ((), ())), preferred_element_type=F32)


def dot_t(a, b):
    return lax.dot_general(a, b, (((1,), (1,)), ((), ())), preferred_element_type=F32)


def t_dot(a, b):
    return lax.dot_general(a, b, (((0,), (0,)), ((), ())), preferred_element_type=F32)


def rms_inv(x):
    return lax.rsqrt(jnp.mean(x * x, axis=-1, keepdims=True) + EPS)


def rms_pull(x, cot):
    r = rms_inv(x)
    return r * cot - x * (r * r * r * jnp.mean(x * cot, axis=-1, keepdims=True))


C0 = 0.7978845608028654
C1 = 0.044715


def gelu_parts(h):
    h2 = h * h
    t = jnp.tanh(h * (C0 + (C0 * C1) * h2))
    half = 0.5 * (1.0 + t)
    grad = half + (0.5 * h) * (1.0 - t * t) * (C0 + (3.0 * C0 * C1) * h2)
    return h * half, grad


def attend(qkv, d_heads, seq):
    rows, w3 = qkv.shape
    width = w3 // 3
    head = width // 2
    scale = head ** -0.5
    low = lax.broadcasted_iota(jnp.int32, (seq, width), 1) < head
    outs, grads = [], []
    for s in range(rows // seq):
        block = qkv[s * seq : (s + 1) * seq]
        qf = block[:, :width]
        q = qf.astype(BF)
        k = block[:, width : 2 * width].astype(BF)
        v = block[:, 2 * width :].astype(BF)
        if d_heads is not None:
            dof = d_heads[s * seq : (s + 1) * seq]
            do = dof.astype(BF)
        o_h, dq_h, dk_h, dv_h = [], [], [], []
        for h in range(2):
            mask = low if h == 0 else jnp.logical_not(low)
            q_m = jnp.where(mask, qf, 0.0).astype(BF)
            scores = dot_t(q_m, k) * scale
            e = jnp.exp(scores - jnp.max(scores, axis=-1, keepdims=True))
            probs = e * (1.0 / jnp.sum(e, axis=-1, keepdims=True))
            probs_b = probs.astype(BF)
            o_h.append(dot(probs_b, v))
            if d_heads is not None:
                do_m = jnp.where(mask, dof, 0.0).astype(BF)
                d_probs = dot_t(do_m, v)
                delta = jnp.sum(d_probs * probs, axis=-1, keepdims=True)
                ds = (probs * (d_probs - delta) * scale).astype(BF)
                dv_h.append(t_dot(probs_b, do))
                dq_h.append(dot(ds, k))
                dk_h.append(t_dot(ds, q))
        pick = lambda pair: jnp.where(low, pair[0], pair[1]).astype(BF)
        outs.append(pick(o_h))
        if d_heads is not None:
            grads.append(jnp.concatenate([pick(dq_h), pick(dk_h), pick(dv_h)], axis=1))
    o = jnp.concatenate(outs, axis=0)
    return o, (jnp.concatenate(grads, axis=0) if grads else None)


def call(body, grid, in_specs, out_specs, out_shape, scratch, sp, args, flops, nbytes, aliases=None):
    n_sp = 1
    return pl.pallas_call(
        body,
        grid_spec=pltpu.PrefetchScalarGridSpec(
            num_scalar_prefetch=n_sp, grid=grid, in_specs=in_specs, out_specs=out_specs, scratch_shapes=scratch
        ),
        out_shape=out_shape,
        input_output_aliases=aliases or {},
        compiler_params=pltpu.CompilerParams(
            dimension_semantics=("arbitrary",) * len(grid), vmem_limit_bytes=VMEM
        ),
        cost_estimate=pl.CostEstimate(flops=int(flops), bytes_accessed=int(nbytes), transcendentals=0),
    )(sp, *args)


def g_chain(sp, x, x_idx, d2, d2_idx, d1, d1_idx, weights, n_blk):
    rows, hid = d1.shape[1:]
    wr = weights.shape[1] // n_blk
    ff = wr // 2

    def body(sp_ref, x_ref, d2_ref, d1_ref, w_ref, out_ref, outb_ref, g_s, acc_s):
        step = pl.program_id(0)

        @pl.when(step == 0)
        def _():
            x_v = x_ref[0]
            g_s[...] = (x_v * rms_inv(x_v)).astype(BF)
            acc_s[...] = jnp.zeros_like(acc_s)

        w_in = w_ref[0, :ff]
        _, grad = gelu_parts(dot_t(g_s[...], w_in))
        d_act = dot_t(d2_ref[0].astype(BF), w_ref[0, ff:])
        acc_s[...] += dot((d_act * grad).astype(BF), w_in)

        @pl.when(step == N * n_blk - 1)
        def _():
            new = d1_ref[0] + rms_pull(x_ref[0], acc_s[...])
            out_ref[0] = new
            outb_ref[0] = new.astype(BF)

    tile = (1, rows, hid)
    return call(
        body,
        (N * n_blk,),
        [
            pl.BlockSpec(tile, lambda s, sp: (x_idx(sp), 0, 0)),
            pl.BlockSpec(tile, lambda s, sp: (d2_idx(sp, s // N), 0, 0)),
            pl.BlockSpec(tile, lambda s, sp: (d1_idx(sp), 0, 0)),
            pl.BlockSpec((1, wr, hid), lambda s, sp: (s % N, s // N, 0)),
        ],
        [pl.BlockSpec(tile, lambda s, sp: (0, 0, 0))] * 2,
        [jax.ShapeDtypeStruct(tile, F32), jax.ShapeDtypeStruct(tile, BF)],
        [pltpu.VMEM((rows, hid), BF), pltpu.VMEM((rows, hid), F32)],
        sp,
        (x, d2, d1, weights),
        6 * rows * hid * ff * N * n_blk,
        weights.size * 2 + 4 * rows * hid * 4,
    )


def f_chain(sp, xs, x_idxs, d1b, d2, d2_idx, weights, seq):
    n_blk = len(xs)
    rows, hid = d2.shape[1:]
    wr = weights.shape[1] // n_blk
    w3 = wr * 3 // 4

    def body(sp_ref, *refs):
        x_refs, (d1_ref, d2_ref, w_ref, out_ref, outb_ref, f_s, acc_s) = refs[:n_blk], refs[n_blk:]
        step = pl.program_id(0)

        @pl.when(step == 0)
        def _():
            out_ref[0] = d2_ref[0]

        for i in range(n_blk):

            @pl.when(step == N * i)
            def _():
                x_v = x_refs[i][0]
                f_s[...] = (x_v * rms_inv(x_v)).astype(BF)
                acc_s[...] = jnp.zeros_like(acc_s)

        w_q = w_ref[0, :w3]
        qkv = dot_t(f_s[...], w_q)
        d_heads = dot_t(d1_ref[0], w_ref[0, w3:])
        _, d_qkv = attend(qkv, d_heads, seq)
        acc_s[...] += dot(d_qkv, w_q)

        for i in range(n_blk):

            @pl.when(step == N * i + N - 1)
            def _():
                new = out_ref[0] + rms_pull(x_refs[i][0], acc_s[...])
                out_ref[0] = new
                outb_ref[0] = new.astype(BF)

    tile = (1, rows, hid)
    x_spec = lambda idx: pl.BlockSpec(tile, lambda s, sp: (idx(sp), 0, 0))
    return call(
        body,
        (N * n_blk,),
        [x_spec(idx) for idx in x_idxs]
        + [
            pl.BlockSpec(tile, lambda s, sp: (0, 0, 0)),
            pl.BlockSpec(tile, lambda s, sp: (d2_idx(sp), 0, 0)),
            pl.BlockSpec((1, wr, hid), lambda s, sp: (s % N, s // N, 0)),
        ],
        [pl.BlockSpec(tile, lambda s, sp: (0, 0, 0)), pl.BlockSpec(tile, lambda s, sp: (s // N, 0, 0))],
        [jax.ShapeDtypeStruct(tile, F32), jax.ShapeDtypeStruct((n_blk, rows, hid), BF)],
        [pltpu.VMEM((rows, hid), BF), pltpu.VMEM((rows, hid), F32)],
        sp,
        (*xs, d1b, d2, weights),
        24e9 * n_blk,
        weights.size * 2 + 6 * rows * hid * 4,
    )


def g_forward(sp, x_one, y_two, weights, blk, n_blk):
    half = N // 2
    per = 2
    rows, hid = x_one.shape[2:]
    wr = weights.shape[1] // n_blk
    ff = wr // 2
    m = per * rows

    def body(sp_ref, x_ref, y_ref, w_ref, out_ref, outb_ref, g_s, acc_s):
        j = pl.program_id(1)

        @pl.when(j == 0)
        def _():
            x_v = x_ref[...].reshape(m, hid)
            g_s[...] = (x_v * rms_inv(x_v)).astype(BF)
            acc_s[...] = jnp.zeros_like(acc_s)

        act, _ = gelu_parts(dot_t(g_s[...], w_ref[0, :ff]))
        acc_s[...] += dot(act.astype(BF), w_ref[0, ff:])

        @pl.when(j == N - 1)
        def _():
            x_two = y_ref[...].reshape(m, hid) - acc_s[...]
            out_ref[...] = x_two.reshape(per, rows, hid)
            outb_ref[...] = (x_two * rms_inv(x_two)).astype(BF).reshape(per, rows, hid)

    tile = (per, 1, rows, hid)
    return call(
        body,
        (half // per, N),
        [
            pl.BlockSpec(tile, lambda i, j, sp: (i, sp[1], 0, 0)),
            pl.BlockSpec(tile, lambda i, j, sp: (i, sp[1], 0, 0)),
            pl.BlockSpec((1, wr, hid), lambda i, j, sp: (j, blk, 0)),
        ],
        [pl.BlockSpec((per, rows, hid), lambda i, j, sp: (i, 0, 0))] * 2,
        [jax.ShapeDtypeStruct((half, rows, hid), F32), jax.ShapeDtypeStruct((half, rows, hid), BF)],
        [pltpu.VMEM((m, hid), BF), pltpu.VMEM((m, hid), F32)],
        sp,
        (x_one, y_two, weights),
        4 * half * rows * hid * ff * N,
        half * rows * hid * 14 + 2 * N * wr * hid * half // per,
    )


def f_forward(sp, f_in, y_one, weights, seq):
    half, rows, hid = f_in.shape
    wr = weights.shape[1]
    w3 = wr * 3 // 4

    def body(sp_ref, f_ref, y_ref, w_ref, out_ref, acc_s):
        j = pl.program_id(1)

        @pl.when(j == 0)
        def _():
            acc_s[...] = jnp.zeros_like(acc_s)

        qkv = dot_t(f_ref[0], w_ref[0, :w3])
        o, _ = attend(qkv, None, seq)
        acc_s[...] += dot(o, w_ref[0, w3:])

        @pl.when(j == N - 1)
        def _():
            out_ref[0] = y_ref[0, 0] - acc_s[...]

    tile = (1, rows, hid)
    return call(
        body,
        (half, N),
        [
            pl.BlockSpec(tile, lambda i, j, sp: (i, 0, 0)),
            pl.BlockSpec((1, 1, rows, hid), lambda i, j, sp: (i, sp[1], 0, 0)),
            pl.BlockSpec((1, wr, hid), lambda i, j, sp: (j, 0, 0)),
        ],
        pl.BlockSpec(tile, lambda i, j, sp: (i, 0, 0)),
        jax.ShapeDtypeStruct((half, rows, hid), F32),
        [pltpu.VMEM((rows, hid), F32)],
        sp,
        (f_in, y_one, weights),
        50e9,
        half * rows * hid * 10 + 2 * N * wr * hid * half,
    )


def g_grads(sp, x_one, d2, d2_idx, w_in, w_out, top_blk, n_blk, prev):
    rows, hid = x_one.shape[1:]
    n_layers, _, ff = w_in.shape

    def body(sp_ref, x_ref, d2_ref, wi_ref, wo_ref, *rest):
        dwi_ref, dwo_ref = rest[-2:]
        t = pl.program_id(1)
        x_v = x_ref[0]
        g = (x_v * rms_inv(x_v)).astype(BF)
        d2_v = d2_ref[...].reshape(rows, hid).astype(BF)
        act, grad = gelu_parts(dot(g, wi_ref[0]))
        d_hidden = (dot_t(d2_v, wo_ref[0]) * grad).astype(BF)
        dwi = t_dot(g, d_hidden)
        dwo = t_dot(act.astype(BF), d2_v)

        @pl.when(t == 0)
        def _():
            dwi_ref[0] = dwi
            dwo_ref[0] = dwo

        @pl.when(t > 0)
        def _():
            dwi_ref[0] += dwi
            dwo_ref[0] += dwo

    any_spec = pl.BlockSpec(memory_space=pl.ANY)
    d2_tile = (1,) * (d2.ndim - 2) + (rows, hid)
    return call(
        body,
        (n_blk, N),
        [
            pl.BlockSpec((1, rows, hid), lambda b, t, sp: (t, 0, 0)),
            pl.BlockSpec(d2_tile, lambda b, t, sp: d2_idx(b, t)),
            pl.BlockSpec((1, hid, ff), lambda b, t, sp: (top_blk - b, 0, 0)),
            pl.BlockSpec((1, ff, hid), lambda b, t, sp: (top_blk - b, 0, 0)),
        ]
        + [any_spec] * len(prev),
        [
            pl.BlockSpec((1, hid, ff), lambda b, t, sp: (top_blk - b, 0, 0)),
            pl.BlockSpec((1, ff, hid), lambda b, t, sp: (top_blk - b, 0, 0)),
        ],
        [jax.ShapeDtypeStruct((n_layers, hid, ff), F32), jax.ShapeDtypeStruct((n_layers, ff, hid), F32)],
        [],
        sp,
        (x_one, d2, w_in, w_out, *prev),
        8 * N * rows * hid * ff * n_blk,
        n_blk * N * rows * hid * 6,
        {5 + i: i for i in range(len(prev))},
    )


def f_grads(sp, f_ins, d1, w_qkv, w_o, blk, prev, seq):
    rows, hid = d1.shape[1:]
    n_layers, w3, _ = w_qkv.shape
    w1 = w_o.shape[1]
    half = N // 2
    two = len(f_ins) == 2

    def body(sp_ref, *refs):
        d1_ref, wq_ref, wo_ref = refs[len(f_ins) : len(f_ins) + 3]
        dwq_ref, dwo_ref, f_s = refs[-3:]
        t = pl.program_id(0)
        if two:

            @pl.when(t < half)
            def _():
                f_s[...] = refs[0][0]

            @pl.when(t >= half)
            def _():
                f_s[...] = refs[1][0]
        else:
            x_v = refs[0][0]
            f_s[...] = (x_v * rms_inv(x_v)).astype(BF)
        d1_v = d1_ref[0].astype(BF)
        qkv = dot_t(f_s[...], wq_ref[0])
        d_heads = dot_t(d1_v, wo_ref[0])
        o, d_qkv = attend(qkv, d_heads, seq)
        dwq = t_dot(d_qkv, f_s[...])
        dwo = t_dot(o, d1_v)

        @pl.when(t == 0)
        def _():
            dwq_ref[0] = dwq
            dwo_ref[0] = dwo

        @pl.when(t > 0)
        def _():
            dwq_ref[0] += dwq
            dwo_ref[0] += dwo

    any_spec = pl.BlockSpec(memory_space=pl.ANY)
    tile = (1, rows, hid)
    if two:
        f_specs = [
            pl.BlockSpec(tile, lambda t, sp: (jnp.minimum(t, half - 1), 0, 0)),
            pl.BlockSpec(tile, lambda t, sp: (jnp.maximum(t - half, 0), 0, 0)),
        ]
        d1_spec = pl.BlockSpec(tile, lambda t, sp: (2 * (t % half) + (t // half + sp[1]) % 2, 0, 0))
    else:
        f_specs = [pl.BlockSpec(tile, lambda t, sp: (t, 0, 0))]
        d1_spec = pl.BlockSpec(tile, lambda t, sp: (t, 0, 0))
    w_spec = lambda w: pl.BlockSpec((1, w, hid), lambda t, sp: (blk, 0, 0))
    n_in = len(f_ins) + 3
    return call(
        body,
        (N,),
        f_specs + [d1_spec, w_spec(w3), w_spec(w1)] + [any_spec] * len(prev),
        [w_spec(w3), w_spec(w1)],
        [jax.ShapeDtypeStruct((n_layers, w3, hid), F32), jax.ShapeDtypeStruct((n_layers, w1, hid), F32)],
        [pltpu.VMEM((rows, hid), BF)],
        sp,
        (*f_ins, d1, w_qkv, w_o, *prev),
        28e9,
        N * rows * hid * 6,
        {1 + n_in + i: i for i in range(len(prev))},
    )


def solution(mesh):
    act_spec = P("dp", None, None)
    saved_spec = P(None, "dp", None, None)
    weight_specs = (P(None, None, None, "tp", None), P(None, "tp", None, None), P(None, None, "tp"), P(None, "tp", None))
    grad_specs = (P("dp", None, None, "tp", None), P("dp", "tp", None, None), P("dp", None, "tp"), P("dp", "tp", None))
    core_pairs = [(i, i ^ 1) for i in range(N)]

    def gather(x):
        return lax.all_gather(x, "tp", axis=0, tiled=False)

    def per_device(y_one, y_two, dy_one, dy_two, saved_one, saved_two, w_qkv, w_o, w_in, w_out):
        seqs, seq, hid = y_one.shape
        n_layers = w_qkv.shape[0]
        n_pairs = saved_one.shape[0]
        rows = seqs * seq // N
        me = lax.axis_index("tp")
        core = me % 2
        sp = jnp.stack([me, core, me // 2]).astype(jnp.int32)

        tiles = lambda x: x.reshape(N, rows, hid)
        pairs = lambda x: x.reshape(N // 2, 2, rows, hid)
        own = lambda sp: sp[0]
        in_half = lambda sp: sp[2]
        first = lambda sp: 0

        wq_t = jnp.transpose(w_qkv, (0, 2, 3, 4, 1)).reshape(n_layers, -1, hid)
        wo_t = w_o.reshape(n_layers, -1, hid)
        g_bundle = lambda b: jnp.concatenate([w_in[b].T, w_out[b]], axis=0)
        f_bundle = lambda b: jnp.concatenate([wq_t[b], wo_t[b]], axis=0)

        def swap(x):
            return lax.ppermute(x, "tp", core_pairs)

        def whole(half_own):
            other = swap(half_own)
            even = jnp.where(core == 0, half_own, other)
            odd = jnp.where(core == 0, other, half_own)
            return jnp.stack([even, odd], axis=1).reshape(seqs, seq, hid)

        top = n_layers - 1
        wg = gather(g_bundle(top))
        wf = gather(jnp.concatenate([f_bundle(top), f_bundle(top - 1)], axis=0)) if n_pairs else gather(f_bundle(0))
        g_acc = g_grads(sp, tiles(y_one), tiles(dy_two), lambda b, t: (t, 0, 0), w_in, w_out, top, 1, ())
        x2h, f_h = g_forward(sp, pairs(y_one), pairs(y_two), wg, 0, 1)
        d1, d1b = g_chain(
            sp, tiles(y_one), own, tiles(dy_two), lambda sp, b: sp[0], tiles(dy_one), own, wg, 1
        )
        d2, d2_idx = tiles(dy_two), own
        f_acc = ()
        y1 = y_one
        for pair in reversed(range(n_pairs)):
            rev = 2 * pair + 2
            s_one, s_two = saved_one[pair], saved_two[pair]
            d1_all = gather(d1b[0])
            wg = gather(jnp.concatenate([g_bundle(rev - 1), g_bundle(rev - 2)], axis=0))
            d2, d2b = f_chain(sp, (x2h, tiles(s_two)), (in_half, own), d1b, d2, d2_idx, wf, seq)
            d2_idx = first
            nxt = rev - 2
            wf = gather(f_bundle(0)) if pair == 0 else gather(jnp.concatenate([f_bundle(nxt), f_bundle(nxt - 1)], axis=0))
            d2_all = gather(d2b)
            f_acc = f_grads(sp, (f_h, swap(f_h)), d1_all, wq_t, wo_t, rev, f_acc, seq)
            f_acc = f_grads(sp, (tiles(s_two),), d1_all, wq_t, wo_t, rev - 1, f_acc, seq)
            x2h, f_h = g_forward(sp, pairs(s_one), pairs(s_two), wg, 1, 2)
            d1, d1b = g_chain(sp, tiles(s_one), own, d2b, lambda sp, b: b, d1, first, wg, 2)
            g_acc = g_grads(
                sp, tiles(s_one), d2_all, lambda b, t: (t, b, 0, 0), w_in, w_out, rev - 1, 2, g_acc
            )
            y1 = s_one
        d1_all = gather(d1[0])
        x_two = whole(x2h)
        x_one = whole(f_forward(sp, f_h, pairs(y1), wf, seq))
        d2, _ = f_chain(sp, (x2h,), (in_half,), d1b, d2, d2_idx, wf, seq)
        d2_all = gather(d2[0])
        f_acc = f_grads(sp, (f_h, swap(f_h)), d1_all, wq_t, wo_t, 0, f_acc, seq)

        head = w_qkv.shape[-1]
        dwq = jnp.transpose(f_acc[0].reshape(n_layers, 3, -1, head, hid), (0, 4, 1, 2, 3))
        dwo = f_acc[1].reshape(w_o.shape)
        shape = (seqs, seq, hid)
        return (x_one, x_two, d1_all.reshape(shape), d2_all.reshape(shape), dwq, dwo) + tuple(g_acc)

    return jax.shard_map(
        per_device,
        mesh=mesh,
        in_specs=(act_spec,) * 4 + (saved_spec,) * 2 + weight_specs,
        out_specs=(act_spec,) * 4 + grad_specs,
        check_vma=False,
    )
```

time: 3550 us -> 1220 us (0.34)
  waiting for transfers between devices: 2350 us -> 227 us
  Pallas kernels: 0 us -> 834 us
  matrix products: 738 us -> 0 us
  other arithmetic: 404 us -> 32.8 us
  local copies, waits for them, and re-layouts: 32.5 us -> 102 us
    psum x6 -> x0, waiting for transfers between devices: 2350 us -> none  [the longest x2 838 us: reversible_block(): x_two = y_two - lax.psum(g_part, 'tp')]
    pallas_call x0 -> x18, Pallas kernels: none -> 834 us  [call(): pl.pallas_call(body, grid_spec=pltpu.PrefetchScalarGridSpec(num_scalar_pr...]
    dot_general x80 -> x0, matrix products: 738 us -> none  [the longest x5 71.4 us: attn_backward(): jnp.einsum('bnqk,bkne->bqne', ds_bf, qkv_all[1], preferred_element_type=j...]
    all_gather x0 -> x12, waiting for transfers between devices: none -> 225 us  [gather(): return lax.all_gather(x, 'tp', axis=0, tiled=False)]
    reduce_sum x13 -> x0, other arithmetic: 166 us -> none  [the longest x6 83.1 us: rms_norm(): state * lax.rsqrt(jnp.mean(state * state, axis=-1, keepdims=True) + EPS)]
    add x4 -> x0, other arithmetic: 119 us -> none  [the longest x2 72.6 us: plain_block(): new_two = d_two + f_norm_pull(lax.psum(f_back, 'tp'))[0]]
    convert_element_type x6 -> x0, other arithmetic: 70.8 us -> none  [the longest x2 55.2 us: attn_backward(): d_bf = d_out.astype(jnp.bfloat16)]
    slice x0 -> x5, local copies, waits for them, and re-layouts: none -> 54 us  [the longest x2 43.8 us: per_device(): s_one, s_two = (saved_one[pair], saved_two[pair])]
  transfers between devices with their start and end apart: 6 -> 17, of which waited for: 6 -> 4; matrix products, arithmetic and copies ran while one was open for 9% -> 8% of each run, Pallas kernels for 0% -> 66%
where the time goes in v1:
time: 1220 us; the launch traced here: 1210 us
  Pallas kernels  834 us (68%)
  waiting for transfers between devices  227 us (19%)
  local copies, waits for them, and re-layouts  102 us (8%)
  other arithmetic  32.8 us (3%)
  between operations  14.8 us (1%)
    pallas_call x18, Pallas kernels, call(): pl.pallas_call(body, grid_spec=pltpu.PrefetchScalarGridSpec(num_scalar_pr...  834 us
    all_gather x12, waiting for transfers between devices, gather(): return lax.all_gather(x, 'tp', axis=0, tiled=False)  225 us
    slice x2, local copies, waits for them, and re-layouts, per_device(): s_one, s_two = (saved_one[pair], saved_two[pair])  43.8 us
    unnamed x17, local copies, waits for them, and re-layouts  30.3 us
  transfers between devices with their start and end apart: 17, of which 4 were waited for; matrix products, arithmetic and copies ran while one was open for 8% of the time, Pallas kernels for 66%

profile of v1, /device:TPU:0, one launch (start us, length us, event | category | flops | bytes accessed | tf_op | source)
XLA Modules:
  0.0 1212.4 jit_solution(9530898879336836583)
XLA Ops:
  7.2 4.3 fusion.2
  13.8 4.8 slice_bitcast_fusion
  45.3 61.9 %all-gather.35.cloned.1.call-done = bf16[8192,1024]{1,0:T(8,128)(2,1)} async-done(((bf16[1024,1024]{1,0:T(8,128)(2,1)}), bf16[8192,1024]{1,0:T(8,128)(2,1)}) %all-gather.35.cloned.1.call-update) | async-done | bytes 16777232 | tf_op jit(solution)/shard_map/all_gather | solution.py:420
  107.2 22.7 %shard_map.165 = (f32[1,512,1024]{2,1,0:T(8,128)}, bf16[1,512,1024]{2,1,0:T(8,128)(2,1)}) custom-call(s32[3]{0:T(128)} %pad_add_fusion.sp_ref, f32[8,512,1024]{2,1,0:T(8,128)} %bitcast.80, f32[8,512,1024]{2,1,0:T(8,128)} %bitcast.83, f32[8,512,1024]{2,1,0:T(8,128)} %bitcast.79, bf16[8,1024,1024]{2,1,0:T(8,128)(2,1)} %bitcast.86), custom_call_target="tpu_custom_call" | custom-call | flops 12884901888 | bytes 25165824 | tf_op jit(solution)/shard_map/pallas_call | solution.py:93
  130.1 21.9 %fusion = (f32[1,16,256,1024]{3,2,1,0:T(8,128)}, f32[1,16,256,1024]{3,2,1,0:T(8,128)}) fusion(f32[2,16,256,1024]{3,2,1,0:T(8,128)} %param.15), kind=kLoop, calls=%fused_computation.18 | loop fusion | bytes 67108864 | tf_op jit(solution)/shard_map/slice | solution.py:464
  151.9 54.1 %shard_map.164 = (f32[4,512,1024]{2,1,0:T(8,128)}, bf16[4,512,1024]{2,1,0:T(8,128)(2,1)}) custom-call(s32[3]{0:T(128)} %pad_add_fusion.sp_ref, f32[4,2,512,1024]{3,2,1,0:T(8,128)} %bitcast.81, f32[4,2,512,1024]{3,2,1,0:T(8,128)} %bitcast.135, bf16[8,1024,1024]{2,1,0:T(8,128)(2,1)} %bitcast.87), custom_call_target="tpu_custom_call" | custom-call | flops 34359738368 | bytes 62914560 | tf_op jit(solution)/shard_map/pallas_call | solution.py:93
  206.1 71.8 %shard_map.166 = (f32[1,512,1024]{2,1,0:T(8,128)}, bf16[2,512,1024]{2,1,0:T(8,128)(2,1)}) custom-call(s32[3]{0:T(128)} %pad_add_fusion.sp_ref, f32[4,512,1024]{2,1,0:T(8,128)} %get-tuple-element.44.refs_0_, f32[8,512,1024]{2,1,0:T(8,128)} %bitcast.99, bf16[1,512,1024]{2,1,0:T(8,128)(2,1)} %get-tuple-element.45.refs_2_, f32[8,512,1024]{2,1,0:T(8,128)} %bitcast.84, ...), custom_call_target="tpu_custom_call" | custom-call | flops 48000000000 | bytes 29360128 | tf_op jit(solution)/shard_map/pallas_call | solution.py:93
  278.2 21.9 %fusion.1 = (f32[1,16,256,1024]{3,2,1,0:T(8,128)}, f32[1,16,256,1024]{3,2,1,0:T(8,128)}) fusion(f32[2,16,256,1024]{3,2,1,0:T(8,128)} %param.14), kind=kLoop, calls=%fused_computation.19 | loop fusion | bytes 67108864 | tf_op jit(solution)/shard_map/slice | solution.py:464
  300.1 51.2 %all-gather.33.cloned.1.call-done = bf16[16384,1024]{1,0:T(8,128)(2,1)} async-done(((bf16[2048,1024]{1,0:T(8,128)(2,1)}), bf16[16384,1024]{1,0:T(8,128)(2,1)}) %all-gather.33.cloned.1.call-update) | async-done | bytes 33554448 | tf_op jit(solution)/shard_map/all_gather | solution.py:420
  351.3 38.3 %shard_map.167 = (f32[1,512,1024]{2,1,0:T(8,128)}, bf16[1,512,1024]{2,1,0:T(8,128)(2,1)}) custom-call(s32[3]{0:T(128)} %pad_add_fusion.sp_ref, f32[8,512,1024]{2,1,0:T(8,128)} %bitcast.102, bf16[2,512,1024]{2,1,0:T(8,128)(2,1)} %get-tuple-element.46.d2_ref, f32[1,512,1024]{2,1,0:T(8,128)} %get-tuple-element.47.d1_ref, bf16[8,2048,1024]{2,1,0:T(8,128)(2,1)} %bitcast.131), custom_call_target="tpu_custom_call" | custom-call | flops 25769803776 | bytes 41943040 | tf_op jit(solution)/shard_map/pallas_call | solution.py:93
  389.6 54.1 %shard_map.163 = (f32[4,512,1024]{2,1,0:T(8,128)}, bf16[4,512,1024]{2,1,0:T(8,128)(2,1)}) custom-call(s32[3]{0:T(128)} %pad_add_fusion.sp_ref, f32[4,2,512,1024]{3,2,1,0:T(8,128)} %bitcast.103, f32[4,2,512,1024]{3,2,1,0:T(8,128)} %bitcast.100, bf16[8,2048,1024]{2,1,0:T(8,128)(2,1)} %bitcast.132), custom_call_target="tpu_custom_call" | custom-call | flops 34359738368 | bytes 62914560 | tf_op jit(solution)/shard_map/pallas_call | solution.py:93
  443.8 71.7 %shard_map.168 = (f32[1,512,1024]{2,1,0:T(8,128)}, bf16[2,512,1024]{2,1,0:T(8,128)(2,1)}) custom-call(s32[3]{0:T(128)} %pad_add_fusion.sp_ref, f32[4,512,1024]{2,1,0:T(8,128)} %get-tuple-element.43.refs_0_, f32[8,512,1024]{2,1,0:T(8,128)} %bitcast.92, bf16[1,512,1024]{2,1,0:T(8,128)(2,1)} %get-tuple-element.48.refs_2_, ...), custom_call_target="tpu_custom_call" | custom-call | flops 48000000000 | bytes 29360128 | tf_op jit(solution)/shard_map/pallas_call | solution.py:93
  515.4 79.1 %all-gather.29.cloned.1.call-done = bf16[16384,1024]{1,0:T(8,128)(2,1)} async-done(((bf16[2048,1024]{1,0:T(8,128)(2,1)}), bf16[16384,1024]{1,0:T(8,128)(2,1)}) %all-gather.29.cloned.1.call-update) | async-done | bytes 33554448 | tf_op jit(solution)/shard_map/all_gather | solution.py:420
  594.6 38.6 %shard_map.169 = (f32[1,512,1024]{2,1,0:T(8,128)}, bf16[1,512,1024]{2,1,0:T(8,128)(2,1)}) custom-call(s32[3]{0:T(128)} %pad_add_fusion.sp_ref, f32[8,512,1024]{2,1,0:T(8,128)} %bitcast.95, bf16[2,512,1024]{2,1,0:T(8,128)(2,1)} %get-tuple-element.50.d2_ref, f32[1,512,1024]{2,1,0:T(8,128)} %get-tuple-element.51.d1_ref, bf16[8,2048,1024]{2,1,0:T(8,128)(2,1)} %bitcast.133), custom_call_target="tpu_custom_call" | custom-call | flops 25769803776 | bytes 41943040 | tf_op jit(solution)/shard_map/pallas_call | solution.py:93
  633.2 54.1 %shard_map.161 = (f32[4,512,1024]{2,1,0:T(8,128)}, bf16[4,512,1024]{2,1,0:T(8,128)(2,1)}) custom-call(s32[3]{0:T(128)} %pad_add_fusion.sp_ref, f32[4,2,512,1024]{3,2,1,0:T(8,128)} %bitcast.96, f32[4,2,512,1024]{3,2,1,0:T(8,128)} %bitcast.93, bf16[8,2048,1024]{2,1,0:T(8,128)(2,1)} %bitcast.134), custom_call_target="tpu_custom_call" | custom-call | flops 34359738368 | bytes 62914560 | tf_op jit(solution)/shard_map/pallas_call | solution.py:93
  687.3 38.1 %shard_map.170 = (f32[1,512,1024]{2,1,0:T(8,128)}, bf16[1,512,1024]{2,1,0:T(8,128)(2,1)}) custom-call(s32[3]{0:T(128)} %pad_add_fusion.sp_ref, f32[4,512,1024]{2,1,0:T(8,128)} %get-tuple-element.42.refs_0_, bf16[1,512,1024]{2,1,0:T(8,128)(2,1)} %get-tuple-element.53.refs_1_, f32[1,512,1024]{2,1,0:T(8,128)} %get-tuple-element.54.refs_2_, ...), custom_call_target="tpu_custom_call" | custom-call | flops 24000000000 | bytes 20971520 | tf_op jit(solution)/shard_map/pallas_call | solution.py:93
  726.7 30.6 %shard_map.176 = (f32[5,1024,512]{2,1,0:T(8,128)}, f32[5,512,1024]{2,1,0:T(8,128)}) custom-call(s32[3]{0:T(128)} %pad_add_fusion.sp_ref, f32[8,512,1024]{2,1,0:T(8,128)} %bitcast.82, f32[8,512,1024]{2,1,0:T(8,128)} %bitcast.85, bf16[5,1024,512]{2,1,0:T(8,128)(2,1)} %wi_ref.5, bf16[5,512,1024]{2,1,0:T(8,128)(2,1)} %wo_ref.5), custom_call_target="tpu_custom_call" | custom-call | flops 17179869184 | bytes 25165824 | tf_op jit(solution)/shard_map/pallas_call | solution.py:93
  757.9 62.0 %shard_map.162 = f32[4,512,1024]{2,1,0:T(8,128)} custom-call(s32[3]{0:T(128)} %pad_add_fusion.sp_ref, bf16[4,512,1024]{2,1,0:T(8,128)(2,1)} %get-tuple-element.41.f_ref.refs_0_, f32[4,2,512,1024]{3,2,1,0:T(8,128)} %bitcast.97, bf16[8,512,1024]{2,1,0:T(8,128)(2,1)} %bitcast.141), custom_call_target="tpu_custom_call" | custom-call | flops 49999998976 | bytes 54525952 | tf_op jit(solution)/shard_map/pallas_call | solution.py:93
  820.1 37.1 %shard_map.171 = (f32[5,384,1024]{2,1,0:T(8,128)}, f32[5,128,1024]{2,1,0:T(8,128)}) custom-call(s32[3]{0:T(128)} %pad_add_fusion.sp_ref, bf16[4,512,1024]{2,1,0:T(8,128)(2,1)} %get-tuple-element.57.refs_0_, bf16[4,512,1024]{2,1,0:T(8,128)(2,1)} %collective-permute-done.4.refs_1_, bf16[8,512,1024]{2,1,0:T(8,128)(2,1)} %all-gather.27.cloned.1.call-done.refs_2_.refs_1_, ...), custom_call_target="tpu_custom_call" | custom-call | flops 28000000000 | bytes 25165824 | tf_op jit(solution)/shard_map/pallas_call | solution.py:93
  857.1 37.3 %shard_map.172 = (f32[5,384,1024]{2,1,0:T(8,128)}, f32[5,128,1024]{2,1,0:T(8,128)}) custom-call(s32[3]{0:T(128)} %pad_add_fusion.sp_ref, f32[8,512,1024]{2,1,0:T(8,128)} %bitcast.101, bf16[8,512,1024]{2,1,0:T(8,128)(2,1)} %all-gather.27.cloned.1.call-done.refs_2_.refs_1_, ...), custom_call_target="tpu_custom_call", output_to_operand_aliasing={{0}: (5, {}), {1}: (6, {})} | custom-call | flops 28000000000 | bytes 25165824 | tf_op jit(solution)/shard_map/pallas_call | solution.py:93
  895.0 55.8 %shard_map.177 = (f32[5,1024,512]{2,1,0:T(8,128)}, f32[5,512,1024]{2,1,0:T(8,128)}) custom-call(s32[3]{0:T(128)} %pad_add_fusion.sp_ref, f32[8,512,1024]{2,1,0:T(8,128)} %bitcast.104, bf16[8,2,512,1024]{3,2,1,0:T(8,128)(2,1)} %bitcast.137, bf16[5,1024,512]{2,1,0:T(8,128)(2,1)} %wi_ref.5, ...), custom_call_target="tpu_custom_call", output_to_operand_aliasing={{0}: (5, {}), {1}: (6, {})} | custom-call | flops 34359738368 | bytes 50331648 | tf_op jit(solution)/shard_map/pallas_call | solution.py:93
  950.8 6.9 select_bitcast_fusion.1
  959.8 6.2 copy.45
  966.1 6.9 select_bitcast_fusion.3
  975.1 6.2 copy.44
  981.4 37.3 %shard_map.173 = (f32[5,384,1024]{2,1,0:T(8,128)}, f32[5,128,1024]{2,1,0:T(8,128)}) custom-call(s32[3]{0:T(128)} %pad_add_fusion.sp_ref, bf16[4,512,1024]{2,1,0:T(8,128)(2,1)} %get-tuple-element.56.refs_0_, bf16[4,512,1024]{2,1,0:T(8,128)(2,1)} %collective-permute-done.3.refs_1_, ...), custom_call_target="tpu_custom_call", output_to_operand_aliasing={{0}: (6, {}), {1}: (7, {})} | custom-call | flops 28000000000 | bytes 25165824 | tf_op jit(solution)/shard_map/pallas_call | solution.py:93
  1018.7 37.1 %shard_map.174 = (f32[5,384,1024]{2,1,0:T(8,128)}, f32[5,128,1024]{2,1,0:T(8,128)}) custom-call(s32[3]{0:T(128)} %pad_add_fusion.sp_ref, f32[8,512,1024]{2,1,0:T(8,128)} %bitcast.94, bf16[8,512,1024]{2,1,0:T(8,128)(2,1)} %all-gather.25.cloned.1.call-done.refs_2_.refs_1_, ...), custom_call_target="tpu_custom_call", output_to_operand_aliasing={{0}: (5, {}), {1}: (6, {})} | custom-call | flops 28000000000 | bytes 25165824 | tf_op jit(solution)/shard_map/pallas_call | solution.py:93
  1055.8 33.2 %all-gather.41.cloned.1.call-done = bf16[16,512,1024]{2,1,0:T(8,128)(2,1)} async-done(((bf16[2,512,1024]{2,1,0:T(8,128)(2,1)}), bf16[16,512,1024]{2,1,0:T(8,128)(2,1)}) %all-gather.41.cloned.1.call-update) | async-done | bytes 16777232 | tf_op jit(solution)/shard_map/all_gather | solution.py:420
  1089.0 55.8 %shard_map.178 = (f32[5,1024,512]{2,1,0:T(8,128)}, f32[5,512,1024]{2,1,0:T(8,128)}) custom-call(s32[3]{0:T(128)} %pad_add_fusion.sp_ref, f32[8,512,1024]{2,1,0:T(8,128)} %bitcast.98, bf16[8,2,512,1024]{3,2,1,0:T(8,128)(2,1)} %bitcast.139, bf16[5,1024,512]{2,1,0:T(8,128)(2,1)} %wi_ref.5, ...), custom_call_target="tpu_custom_call", output_to_operand_aliasing={{0}: (5, {}), {1}: (6, {})} | custom-call | flops 34359738368 | bytes 50331648 | tf_op jit(solution)/shard_map/pallas_call | solution.py:93
  1144.8 37.6 %shard_map.175 = (f32[5,384,1024]{2,1,0:T(8,128)}, f32[5,128,1024]{2,1,0:T(8,128)}) custom-call(s32[3]{0:T(128)} %pad_add_fusion.sp_ref, bf16[4,512,1024]{2,1,0:T(8,128)(2,1)} %get-tuple-element.41.f_ref.refs_0_, bf16[4,512,1024]{2,1,0:T(8,128)(2,1)} %collective-permute-done.2.refs_1_, ...), custom_call_target="tpu_custom_call", output_to_operand_aliasing={{0}: (6, {}), {1}: (7, {})} | custom-call | flops 28000000000 | bytes 25165824 | tf_op jit(solution)/shard_map/pallas_call | solution.py:93
  1182.4 12.8 %copy.68 = f32[16,256,1024]{2,1,0:T(8,128)} copy(f32[16,256,1024]{2,1,0:T(8,128)} %bitcast.89) | data formatting | bytes 33554432
  1198.9 6.2 copy.69
  (68 shorter events, 39.9 us)
Async XLA Ops:
  7.2 100.0 %all-gather.35.cloned.1.call-start = ((), (), s32[]{:S(2)}) async-start(), calls=%async_computation.7 | async-start | bytes 18874368 | tf_op jit(solution)/shard_map/all_gather | solution.py:420
  13.8 4.8 copy-start.1
  20.1 186.0 %all-gather.37.cloned.1.call-start = ((), (), s32[]{:S(2)}) async-start(), calls=%async_computation.8 | async-start | bytes 18874368 | tf_op jit(solution)/shard_map/all_gather | solution.py:420
  27.6 323.7 %all-gather.33.cloned.1.call-start = ((), (), s32[]{:S(2)}) async-start(), calls=%async_computation.6 | async-start | bytes 37748736 | tf_op jit(solution)/shard_map/all_gather | solution.py:420
  34.9 5.0 copy-start.2
  34.9 408.8 %all-gather.39.cloned.1.call-start = ((), (), s32[]{:S(2)}) async-start(), calls=%async_computation.9 | async-start | bytes 18874368 | tf_op jit(solution)/shard_map/all_gather | solution.py:420
  38.0 556.6 %all-gather.29.cloned.1.call-start = ((), (), s32[]{:S(2)}) async-start(), calls=%async_computation.4 | async-start | bytes 37748736 | tf_op jit(solution)/shard_map/all_gather | solution.py:420
  38.1 5.4 copy-start.4
  39.9 3.6 copy-start.3
  43.4 643.9 %all-gather.31.cloned.1.call-start = ((), (), s32[]{:S(2)}) async-start(), calls=%async_computation.5 | async-start | bytes 9437184 | tf_op jit(solution)/shard_map/all_gather | solution.py:420
  44.6 775.5 %all-gather.27.cloned.1.call-start = ((), (), s32[]{:S(2)}) async-start(), calls=%async_computation.3 | async-start | bytes 9437184 | tf_op jit(solution)/shard_map/all_gather | solution.py:420
  129.9 765.1 %all-gather.43.cloned.1.call-start = ((), (), s32[]{:S(2)}) async-start(), calls=%async_computation.11 | async-start | bytes 18874368 | tf_op jit(solution)/shard_map/all_gather | solution.py:420
  277.9 703.5 %all-gather.25.cloned.1.call-start = ((), (), s32[]{:S(2)}) async-start(), calls=%async_computation.2 | async-start | bytes 9437184 | tf_op jit(solution)/shard_map/all_gather | solution.py:420
  389.6 666.2 %all-gather.23.cloned.1.call-start = ((), (), s32[]{:S(2)}) async-start(), calls=%async_computation.1 | async-start | bytes 18874368 | tf_op jit(solution)/shard_map/all_gather | solution.py:420
  725.4 330.4 %all-gather.21.cloned.1.call-start = ((), (), s32[]{:S(2)}) async-start(), calls=%async_computation | async-start | bytes 18874368 | tf_op jit(solution)/shard_map/all_gather | solution.py:420
  726.2 362.8 %all-gather.41.cloned.1.call-start = ((), (), s32[]{:S(2)}) async-start(), calls=%async_computation.10 | async-start | bytes 18874368 | tf_op jit(solution)/shard_map/all_gather | solution.py:420
  757.4 62.7 %collective-permute-start.4 = (bf16[4,512,1024]{2,1,0:T(8,128)(2,1)}, bf16[4,512,1024]{2,1,0:T(8,128)(2,1)}, u32[]{:S(2)}, u32[]{:S(2)}) collective-permute-start(bf16[4,512,1024]{2,1,0:T(8,128)(2,1)} %get-tuple-element.57.refs_0_), channel_id=1, source_target_pairs={{0,1},{1,0},{2,3},{3,2},{4,5},{5,4},{6,7},{7,6}} | collective-permute-start | bytes 12582920 | tf_op jit(solution)/shard_map/ppermute | solution.py:443
  757.6 193.2 %collective-permute-start.1 = (f32[4,512,1024]{2,1,0:T(8,128)}, f32[4,512,1024]{2,1,0:T(8,128)}, u32[]{:S(2)}, u32[]{:S(2)}) collective-permute-start(f32[4,512,1024]{2,1,0:T(8,128)} %get-tuple-element.42.refs_0_), channel_id=1, source_target_pairs={{0,1},{1,0},{2,3},{3,2},{4,5},{5,4},{6,7},{7,6}} | collective-permute-start | bytes 25165832 | tf_op jit(solution)/shard_map/ppermute | solution.py:443
  819.8 146.3 %collective-permute-start = (f32[4,512,1024]{2,1,0:T(8,128)}, f32[4,512,1024]{2,1,0:T(8,128)}, u32[]{:S(2)}, u32[]{:S(2)}) collective-permute-start(f32[4,512,1024]{2,1,0:T(8,128)} %shard_map.162), channel_id=1, source_target_pairs={{0,1},{1,0},{2,3},{3,2},{4,5},{5,4},{6,7},{7,6}} | collective-permute-start | bytes 25165832 | tf_op jit(solution)/shard_map/ppermute | solution.py:443
  894.4 250.4 %collective-permute-start.2 = (bf16[4,512,1024]{2,1,0:T(8,128)(2,1)}, bf16[4,512,1024]{2,1,0:T(8,128)(2,1)}, u32[]{:S(2)}, u32[]{:S(2)}) collective-permute-start(bf16[4,512,1024]{2,1,0:T(8,128)(2,1)} %get-tuple-element.41.f_ref.refs_0_), channel_id=1, source_target_pairs={{0,1},{1,0},{2,3},{3,2},{4,5},{5,4},{6,7},{7,6}} | collective-permute-start | bytes 12582920 | tf_op jit(solution)/shard_map/ppermute | solution.py:443
  894.7 86.7 %collective-permute-start.3 = (bf16[4,512,1024]{2,1,0:T(8,128)(2,1)}, bf16[4,512,1024]{2,1,0:T(8,128)(2,1)}, u32[]{:S(2)}, u32[]{:S(2)}) collective-permute-start(bf16[4,512,1024]{2,1,0:T(8,128)(2,1)} %get-tuple-element.56.refs_0_), channel_id=1, source_target_pairs={{0,1},{1,0},{2,3},{3,2},{4,5},{5,4},{6,7},{7,6}} | collective-permute-start | bytes 12582920 | tf_op jit(solution)/shard_map/ppermute | solution.py:443
  1182.4 16.4 %copy-start = (f32[8,512,1024]{2,1,0:T(8,128)S(1)}, f32[8,512,1024]{2,1,0:T(8,128)}, u32[]{:S(2)}) copy-start(f32[8,512,1024]{2,1,0:T(8,128)} %all-gather.23.cloned.1.call-done) | copy-start | bytes 50331652
Sparse Core Ops, SparseCore 0:
  20.2 86.8 all-gather.34
  109.5 84.0 all-gather.36
  196.0 155.2 all-gather.32
  353.0 84.0 all-gather.38
  439.3 155.2 all-gather.28
  596.2 48.3 all-gather.30
  646.4 48.3 all-gather.26
  696.6 84.0 all-gather.42
  782.6 48.8 all-gather.24
  833.2 84.0 all-gather.22
  919.1 84.0 all-gather.20
  1004.9 84.0 all-gather.40
